TPU v7x, 128 devices: a whole 4x4x4 slice. The times are simulated.
128 devices in a mesh: section: 8 (over z, core), tp: 16 (over x, y).
Axes of the slice: x: 4, y: 4, z: 4, core: 2. Of those that a mesh axis runs over, the one named last changes fastest.
Arguments:
- latents: bfloat16 [1024, 16, 2048], P('tp', 'section'), may hold values from -6 to 6
- timestep: int32 [16], replicated, may hold values from 0 to 999
- target: int32 [16], replicated, may hold values from 0 to 7, as said below
- qkv_weight: bfloat16 [8, 2048, 3, 2048], P('section', None, None, 'tp'), may hold values from -0.125 to 0.125
- mod_weight: bfloat16 [8, 256, 3, 2048], P('section'), may hold values from -2.6 to 2.6
- out_weight: bfloat16 [8, 2048, 2048], P('section', 'tp'), may hold values from -0.125 to 0.125
Outputs:
- updated: bfloat16 [1024, 16, 2048], P('tp', 'section')
Inputs may be any that keep to these rules, and one draw needn't show every extreme that they name: target[l] is l // 2 or l // 2 + 1; of one section's 2 latents at most 1 name the next section, exactly 1 for section 0, none for the last section.
All inputs are finite; a program needn't handle non-finite values.
Results may differ from a plain program's by a relative error of at most 0.023.
Values may be sent and summed in bfloat16 or wider, within the bound.
A program may use at most 128 MiB of HBM per device.

v0:
```python
import math

import jax
import jax.numpy as jnp
from jax import lax
from jax.sharding import PartitionSpec as P

HEAD_DIM = 128
FREQ = 256
MOVE_MAX = 1


def from_behind(shard, axis, by):
    peers = lax.axis_size(axis)
    pairs = [(i, i + by) for i in range(peers) if 0 <= i + by < peers]
    return lax.ppermute(shard, axis, pairs)


def time_embed(steps):
    half_width = FREQ // 2
    frequency = jnp.exp(-math.log(10000.0) * jnp.arange(half_width, dtype=jnp.float32) / half_width)
    angles = steps.astype(jnp.float32)[:, None] * frequency[None, :]
    return jnp.concatenate([jnp.cos(angles), jnp.sin(angles)], axis=1)


def modulate(steps, mod_table):
    feature = jax.nn.silu(time_embed(steps))
    return jnp.einsum(
        "bf,fcd->bcd", feature, mod_table.astype(jnp.float32), precision=lax.Precision.HIGHEST
    )


def normalize(values, shift, scale):
    row_mean = jnp.mean(values, axis=-1, keepdims=True)
    centred = values - row_mean
    variance = jnp.mean(centred * centred, axis=-1, keepdims=True)
    return centred * lax.rsqrt(variance + 1e-06) * (1.0 + scale) + shift


def expert_block(batch, steps, qkv_local, mod_table, out_local):
    mods = modulate(steps, mod_table)
    values = batch.astype(jnp.float32)
    hidden = normalize(values, mods[None, :, 0], mods[None, :, 1]).astype(jnp.bfloat16)
    packed = jnp.einsum(
        "sbd,dce->sbce",
        lax.all_gather(hidden, "tp", axis=0, tiled=True),
        qkv_local,
        preferred_element_type=jnp.float32,
    ).astype(jnp.bfloat16)
    tok_all = packed.shape[0]
    slot_count = packed.shape[1]
    local_width = packed.shape[3]
    head_local = local_width // HEAD_DIM
    split_heads = packed.reshape(tok_all, slot_count, 3, head_local, HEAD_DIM)
    query = split_heads[:, :, 0]
    keys_now = split_heads[:, :, 1]
    vals_now = split_heads[:, :, 2]
    scores = jnp.einsum(
        "qbhe,kbhe->bhqk", query, keys_now, preferred_element_type=jnp.float32
    ) * HEAD_DIM ** (-0.5)
    soft = jax.nn.softmax(scores, axis=-1).astype(jnp.bfloat16)
    mixed = jnp.einsum("bhqk,kbhe->qbhe", soft, vals_now, preferred_element_type=jnp.float32)
    mixed = mixed.astype(jnp.bfloat16).reshape(tok_all, slot_count, local_width)
    proj = lax.psum_scatter(
        jnp.einsum("sbk,kd->sbd", mixed, out_local, preferred_element_type=jnp.float32).astype(
            jnp.bfloat16
        ),
        "tp",
        scatter_dimension=0,
        tiled=True,
    ).astype(jnp.float32)
    return (values + mods[None, :, 2] * proj).astype(jnp.bfloat16)


def movers_first(move_flags, slots):
    order_keys = jnp.where(move_flags, 0, 1).astype(jnp.int32) * slots + jnp.arange(
        slots, dtype=jnp.int32
    )
    return jnp.argsort(order_keys)[:MOVE_MAX]


def body(latents, timestep, target, qkv_weight, mod_weight, out_weight):
    slots = latents.shape[1]
    home_section = lax.axis_index("section")
    prev_section = jnp.maximum(home_section - 1, 0)
    own_steps = lax.dynamic_slice_in_dim(timestep, home_section * slots, slots)
    own_target = lax.dynamic_slice_in_dim(target, home_section * slots, slots)
    prev_steps = lax.dynamic_slice_in_dim(timestep, prev_section * slots, slots)
    prev_target = lax.dynamic_slice_in_dim(target, prev_section * slots, slots)
    own_move = own_target != home_section
    prev_move = prev_target == home_section
    qkv_local = qkv_weight[0]
    mod_table = mod_weight[0]
    out_local = out_weight[0]
    own_order = movers_first(own_move, slots)
    prev_order = movers_first(prev_move, slots)
    outgoing = jnp.take(latents, own_order, axis=1)
    incoming = from_behind(outgoing, "section", 1)
    batch = jnp.concatenate([latents, incoming], axis=1)
    steps = jnp.concatenate([own_steps, jnp.take(prev_steps, prev_order, axis=0)], axis=0)
    result = expert_block(batch, steps, qkv_local, mod_table, out_local)
    coming_back = from_behind(result[:, slots:], "section", -1)
    placing = own_order[None, :] == jnp.arange(slots, dtype=jnp.int32)[:, None]
    returned = jnp.einsum(
        "lm,sme->sle", placing.astype(jnp.bfloat16), coming_back, preferred_element_type=jnp.float32
    ).astype(jnp.bfloat16)
    return jnp.where(own_move[None, :, None], returned, result[:, :slots])


def solution(mesh):
    return jax.shard_map(
        body,
        mesh=mesh,
        in_specs=(
            P("tp", "section", None),
            P(),
            P(),
            P("section", None, None, "tp"),
            P("section", None, None, None),
            P("section", "tp", None),
        ),
        out_specs=P("tp", "section", None),
        check_vma=False,
    )
```

profile of v0, /device:TPU:1, one launch (start us, length us, event | category | flops | bytes accessed | tf_op | source)
XLA Modules:
  0.0 258.3 jit_solution(6811928399783581988)
XLA Ops:
  6.5 0.0 copy-start
  6.5 0.0 all-gather.2.cloned.1.call-start
  6.5 0.9 iota_add_fusion
  7.4 0.6 sort.31
  8.2 1.2 copy.8
  9.4 0.0 copy-start.1
  9.4 0.8 copy-done.1
  10.2 0.7 dynamic-slice_select_fusion
  10.9 4.9 %collective-permute-start = (bf16[64,1,2048]{2,0,1:T(8,128)(2,1)}, bf16[64,1,2048]{2,0,1:T(8,128)(2,1)S(1)}, u32[]{:S(2)}, u32[]{:S(2)}) collective-permute-start(bf16[64,1,2048]{2,0,1:T(8,128)(2,1)} %dynamic-slice_select_fusion), channel_id=1, source_target_pairs={{0,16},{16,32},{32,48},{48,64},{64,80},{80,96},{96,112},{1,17},{17... | collective-permute-start | bytes 786440 | tf_op jit(solution)/shard_map/ppermute | solution.py:16
  15.8 0.7 sort.32
  16.6 0.7 dynamic_slice.13
  17.4 0.0 copy-start.2
  17.4 1.4 dynamic-slice.6
  19.3 0.1 add_convert_fusion
  19.4 0.1 multiply_cosine_fusion
  19.5 0.0 copy-done
  19.5 1.3 fusion.10
  20.9 0.0 collective-permute-done
  20.9 0.0 copy-done.2
  20.9 0.2 convert_reduce_fusion
  21.1 0.4 fusion.16
  21.5 1.5 fusion.19
  22.9 0.0 all-gather.2.cloned.1.call-update
  23.0 0.2 reduce-scatter.2.cloned.1.call-start
  23.2 90.8 %all-gather.2.cloned.1.call-done = bf16[1024,3,2048]{2,0,1:T(8,128)(2,1)} async-done(((bf16[64,3,2048]{2,0,1:T(8,128)(2,1)}), bf16[1024,3,2048]{2,0,1:T(8,128)(2,1)}) %all-gather.2.cloned.1.call-update) | async-done | bytes 12582928 | tf_op jit(solution)/shard_map/all_gather | solution.py:46
  114.0 11.2 %convert_bitcast_fusion = bf16[1024,3,3,1,128]{4,0,2,1,3:T(8,128)(2,1)} fusion(bf16[1024,3,2048]{2,0,1:T(8,128)(2,1)} %all-gather.2.cloned.1.call-done, bf16[1,2048,3,128]{3,1,2,0:T(8,128)(2,1)} %param.9), kind=kOutput, calls=%fused_computation.16 | convolution fusion | flops 4833017856 | bytes 16515072 | tf_op jit(solution)/shard_map/sbd,dce->sbce/dot_general | solution.py:44
  125.2 9.8 %fusion.39 = (f32[3,1024]{1,0:T(4,128)S(1)}, f32[3,1024,1024]{1,2,0:T(8,128)}) fusion(bf16[1024,3,3,1,128]{4,0,2,1,3:T(8,128)(2,1)} %convert_bitcast_fusion), kind=kOutput, calls=%fused_computation.64 | convolution fusion | flops 814744576 | bytes 14168064 | tf_op jit(solution)/shard_map/sub | solution.py:61
  135.0 10.7 %convolution_convert_fusion = bf16[1024,3,2048]{2,0,1:T(8,128)(2,1)} fusion(f32[3,1024,1024]{1,2,0:T(8,128)} %get-tuple-element.40, f32[3,1024]{1,0:T(4,128)S(1)} %get-tuple-element.39, bf16[1024,3,3,1,128]{4,0,2,1,3:T(8,128)(2,1)} %convert_bitcast_fusion, bf16[1,128,2048]{2,1,0:T(8,128)(2,1)} %param.11), kind=kOutput, calls=%fused_computation.7 | convolution fusion | flops 2428895232 | bytes 26488832 | tf_op jit(solution)/shard_map/sbk,kd->sbd/dot_general | solution.py:65
  145.7 0.0 reduce-scatter.2.cloned.1.call-update
  145.7 94.3 %reduce-scatter.2.cloned.1.call-done = bf16[64,3,2048]{2,0,1:T(8,128)(2,1)} async-done(((bf16[1024,3,2048]{2,0,1:T(8,128)(2,1)}), bf16[64,3,2048]{2,0,1:T(8,128)(2,1)}) %reduce-scatter.2.cloned.1.call-update) | async-done | bytes 786448 | tf_op jit(solution)/shard_map/reduce_scatter | solution.py:64
  240.0 1.6 fusion.20
  241.6 3.1 %collective-permute-start.1 = (bf16[64,1,2048]{2,0,1:T(8,128)(2,1)S(1)}, bf16[64,1,2048]{2,0,1:T(8,128)(2,1)S(1)}, u32[]{:S(2)}, u32[]{:S(2)}) collective-permute-start(bf16[64,1,2048]{2,0,1:T(8,128)(2,1)S(1)} %slice.60), channel_id=1, source_target_pairs={{16,0},{32,16},{48,32},{64,48},{80,64},{96,80},{112,96},{17,1},{33... | collective-permute-start | bytes 786440 | tf_op jit(solution)/shard_map/ppermute | solution.py:16
  244.7 5.2 %collective-permute-done.1 = bf16[64,1,2048]{2,0,1:T(8,128)(2,1)S(1)} collective-permute-done((bf16[64,1,2048]{2,0,1:T(8,128)(2,1)S(1)}, bf16[64,1,2048]{2,0,1:T(8,128)(2,1)S(1)}, u32[]{:S(2)}, u32[]{:S(2)}) %collective-permute-start.1) | collective-permute-done | bytes 262176 | tf_op jit(solution)/shard_map/ppermute | solution.py:16
  249.9 0.2 fusion.26
  250.1 1.3 copy.12
  (9 shorter events, 0.2 us)
Async XLA Ops:
  6.5 13.0 %copy-start = (bf16[1,256,3,2048]{3,1,2,0:T(8,128)(2,1)S(1)}, bf16[1,256,3,2048]{3,1,2,0:T(8,128)(2,1)}, u32[]{:S(2)}) copy-start(bf16[1,256,3,2048]{3,1,2,0:T(8,128)(2,1)} %param.10) | copy-start | bytes 9437188
  6.5 107.5 %all-gather.2.cloned.1.call-start = ((), (), s32[]{:S(2)}) async-start(), calls=%async_computation.1 | async-start | bytes 13369344 | tf_op jit(solution)/shard_map/all_gather | solution.py:46
  9.4 0.8 copy-start.1
  10.9 10.0 %collective-permute-start = (bf16[64,1,2048]{2,0,1:T(8,128)(2,1)}, bf16[64,1,2048]{2,0,1:T(8,128)(2,1)S(1)}, u32[]{:S(2)}, u32[]{:S(2)}) collective-permute-start(bf16[64,1,2048]{2,0,1:T(8,128)(2,1)} %dynamic-slice_select_fusion), channel_id=1, source_target_pairs={{0,16},{16,32},{32,48},{48,64},{64,80},{80,96},{96,112},{1,17},{17... | collective-permute-start | bytes 786440 | tf_op jit(solution)/shard_map/ppermute | solution.py:16
  17.4 3.6 %copy-start.2 = (bf16[64,2,2048]{2,0,1:T(8,128)(2,1)S(1)}, bf16[64,2,2048]{2,0,1:T(8,128)(2,1)}, u32[]{:S(2)}) copy-start(bf16[64,2,2048]{2,0,1:T(8,128)(2,1)} %copy-done.1) | copy-start | bytes 1572868
  23.0 217.1 %reduce-scatter.2.cloned.1.call-start = ((), (), s32[]{:S(2)}) async-start(), calls=%async_computation.2 | async-start | bytes 13369344 | tf_op jit(solution)/shard_map/reduce_scatter | solution.py:64
  241.6 8.3 %collective-permute-start.1 = (bf16[64,1,2048]{2,0,1:T(8,128)(2,1)S(1)}, bf16[64,1,2048]{2,0,1:T(8,128)(2,1)S(1)}, u32[]{:S(2)}, u32[]{:S(2)}) collective-permute-start(bf16[64,1,2048]{2,0,1:T(8,128)(2,1)S(1)} %slice.60), channel_id=1, source_target_pairs={{16,0},{32,16},{48,32},{64,48},{80,64},{96,80},{112,96},{17,1},{33... | collective-permute-start | bytes 786440 | tf_op jit(solution)/shard_map/ppermute | solution.py:16
Sparse Core Ops, SparseCore 0:
  23.1 90.8 all-gather.1
  145.8 94.1 reduce-scatter.1
where the time goes:
time: 259 us; the launch traced here: 258 us
  waiting for transfers between devices  190 us (73%)
  matrix products  33 us (13%)
  between operations  14.4 us (6%)
  starting transfers between devices  8.19 us (3%)
  other arithmetic  6.97 us (3%)
  local copies, waits for them, and re-layouts  5.44 us (2%)
    reduce_scatter x1, waiting for transfers between devices, expert_block(): lax.psum_scatter(jnp.einsum('sbk,kd->sbd', mixed, out_local, preferred_el...  94.3 us
    all_gather x1, waiting for transfers between devices, expert_block(): lax.all_gather(hidden, 'tp', axis=0, tiled=True)  90.8 us
    dot_general x1, matrix products, expert_block(): jnp.einsum('sbd,dce->sbce', lax.all_gather(hidden, 'tp', axis=0, tiled=Tr...  11.2 us
    dot_general x1, matrix products, expert_block(): jnp.einsum('sbk,kd->sbd', mixed, out_local, preferred_element_type=jnp.fl...  10.7 us
    sub x1, matrix products, expert_block(): soft = jax.nn.softmax(scores, axis=-1).astype(jnp.bfloat16)  9.77 us
    ppermute x2, starting transfers between devices, from_behind(): return lax.ppermute(shard, axis, pairs)  7.97 us
  transfers between devices with their start and end apart: 4, of which 3 were waited for; matrix products, arithmetic and copies ran while one was open for 2% of the time, Pallas kernels for 0%

commit v1 on v0

v1 whole, which is shorter than its diff:
```python
import functools
import math

import jax
import jax.numpy as jnp
from jax import lax
from jax.experimental import pallas as pl
from jax.experimental.pallas import tpu as pltpu
from jax.sharding import PartitionSpec as P

HEAD_DIM = 128
FREQ = 256
MESH = pl.DeviceIdType.MESH
BF16 = jnp.bfloat16
F32 = jnp.float32


def time_embed(steps):
    half_width = FREQ // 2
    frequency = jnp.exp(-math.log(10000.0) * jnp.arange(half_width, dtype=F32) / half_width)
    angles = steps.astype(F32)[:, None] * frequency[None, :]
    return jnp.concatenate([jnp.cos(angles), jnp.sin(angles)], axis=1)


def split_feature(steps):
    feature = jax.nn.silu(time_embed(steps))
    high = lax.reduce_precision(feature, 8, 7)
    rest = feature - high
    mid = lax.reduce_precision(rest, 8, 7)
    low = rest - mid
    return jnp.concatenate([high, mid, low, jnp.zeros_like(low)], axis=0).astype(BF16)


def kernel(
    flag_ref, feat_ref, stay_ref, move_ref, mod_hbm, wqkv_hbm, wout_hbm,
    upd_ref,
    mod_v, mods, mod_send, mod_recv, hid_send,
    gath, w2, wo2, wn, wno, ws, wso,
    qkv, part, r3, r2, r1, r0,
    ld_sem, md_s, md_r, z_s, z_r, sw_s, sw_r, tok_s, tok_r, rs_s, rs_r,
):
    sections = lax.axis_size("section")
    tok = stay_ref.shape[0]
    sec = lax.axis_index("section")
    tp = lax.axis_index("tp")
    core = lax.rem(sec, 2)
    x = tp // 4
    y = lax.rem(tp, 4)
    u = jnp.where(core == 0, y, x)
    v = jnp.where(core == 0, x, y)

    def at(uu, vv):
        return jnp.where(core == 0, vv * 4 + uu, uu * 4 + vv)

    def flip(a):
        return a + 1 - 2 * lax.rem(a, 2)

    pair = (sec, at(flip(u), v))
    p1 = (sec, at(3 - u, v))
    p2 = (sec, at(u, flip(v)))
    p3 = (sec, at(u, 3 - v))
    before = (lax.rem(sec + sections - 1, sections), tp)
    after = (lax.rem(sec + 1, sections), tp)
    is_a = (u == 0) | (u == 3)
    moved = flag_ref[0] != 0

    def remote(src, dst, ssem, rsem, peer):
        return pltpu.make_async_remote_copy(
            src_ref=src, dst_ref=dst, send_sem=ssem, recv_sem=rsem,
            device_id=peer, device_id_type=MESH,
        )

    mod_load = pltpu.make_async_copy(mod_hbm, mod_v, ld_sem.at[0])
    mod_load.start()
    loads = [
        pltpu.make_async_copy(wqkv_hbm.at[i], w2.at[i, :, pl.ds(0, HEAD_DIM)], ld_sem.at[1 + i])
        for i in range(3)
    ]
    loads.append(pltpu.make_async_copy(wout_hbm, wo2.at[pl.ds(0, HEAD_DIM)], ld_sem.at[4]))
    for load in loads:
        load.start()

    barrier = pltpu.get_barrier_semaphore()
    for peer in (pair, p1, p2, p3, before, after):
        pl.semaphore_signal(barrier, inc=1, device_id=peer, device_id_type=MESH)
    pl.semaphore_wait(barrier, 6)

    z_copies = [
        remote(wqkv_hbm.at[i], wn.at[i], z_s.at[i], z_r.at[i], before) for i in range(3)
    ]
    z_copies.append(remote(wout_hbm, wno, z_s.at[3], z_r.at[3], before))

    mod_load.wait()
    mod_send[...] = jnp.zeros_like(mod_send)
    for c in range(3):
        prod = jnp.dot(feat_ref[...], mod_v[c], preferred_element_type=F32)
        full = prod[0:8] + prod[8:16] + prod[16:24]
        mods[c] = full
        mod_send[pl.ds(c, 1), :] = full[2:3]
    md = remote(mod_send, mod_recv, md_s, md_r, before)
    md.start()
    for copy in z_copies:
        copy.start()

    def norm(ref, shift, scale):
        values = ref[...].astype(F32)
        centred = values - jnp.mean(values, axis=-1, keepdims=True)
        variance = jnp.mean(centred * centred, axis=-1, keepdims=True)
        return (centred * lax.rsqrt(variance + 1e-06) * (1.0 + scale) + shift).astype(BF16)

    stay_hidden = norm(stay_ref, mods[0, 0:1, :], mods[1, 0:1, :])
    gath[0] = stay_hidden
    hid_send[...] = stay_hidden
    md.wait_recv()
    move_hidden = norm(
        move_ref,
        jnp.where(moved, mod_recv[0:1, :], mods[0, 1:2, :]),
        jnp.where(moved, mod_recv[1:2, :], mods[1, 1:2, :]),
    )
    gath[0] = jnp.where(is_a, gath[0], move_hidden)
    hid_send[...] = jnp.where(is_a, move_hidden, hid_send[...])

    t0 = remote(hid_send, gath.at[1], tok_s.at[0], tok_r.at[0], pair)
    d1 = [remote(gath.at[j], gath.at[2 + j], tok_s.at[1 + j], tok_r.at[1 + j], p1) for j in range(2)]
    d2 = [remote(gath.at[j], gath.at[4 + j], tok_s.at[3 + j], tok_r.at[3 + j], p2) for j in range(4)]
    d3 = [remote(gath.at[j], gath.at[8 + j], tok_s.at[7 + j], tok_r.at[7 + j], p3) for j in range(8)]
    t0.start()
    d1[0].start()
    d2[0].start()
    d3[0].start()

    swaps = [
        remote(ws.at[i], w2.at[i, :, pl.ds(HEAD_DIM, HEAD_DIM)], sw_s.at[i], sw_r.at[i], pair)
        for i in range(3)
    ]
    swaps.append(remote(wso, wo2.at[pl.ds(HEAD_DIM, HEAD_DIM)], sw_s.at[3], sw_r.at[3], pair))
    send_next = is_a & moved
    keep_next = jnp.logical_not(is_a) & moved

    def weight(i):
        loads[i].wait()
        z_copies[i].wait_recv()
        if i < 3:
            rows = w2.shape[1]
            step = min(512, rows)

            def piece(b, carry):
                rs = pl.ds(pl.multiple_of(b * step, step), step)
                own = w2[i, rs, pl.ds(0, HEAD_DIM)]
                nxt = wn[i, rs, :]
                ws[i, rs, :] = jnp.where(send_next, nxt, own)
                w2[i, rs, pl.ds(0, HEAD_DIM)] = jnp.where(keep_next, nxt, own)
                return carry

            lax.fori_loop(0, rows // step, piece, 0)
        else:
            own = wo2[pl.ds(0, HEAD_DIM), :]
            nxt = wno[...]
            wso[...] = jnp.where(send_next, nxt, own)
            wo2[pl.ds(0, HEAD_DIM), :] = jnp.where(keep_next, nxt, own)
        swaps[i].start()

    t0.wait_recv()
    d1[1].start()
    d2[1].start()
    d3[1].start()
    for j in range(2):
        d1[j].wait_recv()
        d2[2 + j].start()
        d3[2 + j].start()
    weight(0)
    for j in range(2):
        d2[j].wait_recv()
        d3[4 + j].start()
    weight(1)
    for j in range(2, 4):
        d2[j].wait_recv()
        d3[4 + j].start()
    weight(2)
    weight(3)
    for j in range(8):
        d3[j].wait_recv()

    slots = 4
    width = slots * tok
    depth = gath.shape[2]

    for i in range(3):
        swaps[i].wait_recv()

        def project(b, carry):
            rows = gath[pl.ds(b * slots, slots)].reshape(width, depth)
            out = jnp.dot(rows, w2[i], preferred_element_type=F32)
            qkv[i, pl.ds(pl.multiple_of(b * width, width), width), :] = out.astype(BF16)
            return carry

        lax.fori_loop(0, 16 // slots, project, 0)
    swaps[3].wait_recv()

    s3 = {j: remote(part.at[j], r3.at[j - 8], rs_s.at[j - 8], rs_r.at[j - 8], p3) for j in range(8, 16)}
    s2 = {j: remote(part.at[j], r2.at[j - 4], rs_s.at[4 + j], rs_r.at[4 + j], p2) for j in range(4, 8)}
    s1 = {j: remote(part.at[j], r1.at[j - 2], rs_s.at[10 + j], rs_r.at[10 + j], p1) for j in range(2, 4)}
    s0 = remote(part.at[1], r0, rs_s.at[14], rs_r.at[14], pair)

    factor = HEAD_DIM ** (-0.5) * math.log2(math.e)
    n_col = 4
    col = depth // n_col

    def attend(b):
        rows = pl.ds(b * width, width)
        heads = []
        for h in range(2):
            lanes = pl.ds(h * HEAD_DIM, HEAD_DIM)
            scores = lax.dot_general(
                qkv[0, rows, lanes], qkv[1, :, lanes], (((1,), (1,)), ((), ())),
                preferred_element_type=F32,
            )
            top = jnp.max(scores, axis=-1, keepdims=True)
            weights = jnp.exp2((scores - top) * factor)
            total = jnp.sum(weights, axis=-1, keepdims=True)
            mixed = jnp.dot(weights.astype(BF16), qkv[2, :, lanes], preferred_element_type=F32)
            heads.append((mixed / total).astype(BF16))
        both = jnp.concatenate(heads, axis=1)
        for n in range(n_col):
            lanes = pl.ds(n * col, col)
            out = jnp.dot(both, wo2[:, lanes], preferred_element_type=F32).astype(BF16)
            part[pl.ds(b * slots, slots), :, lanes] = out.reshape(slots, tok, col)

    for b in (3, 2, 1, 0):
        attend(b)
        if b >= 2:
            for j in reversed(range(b * slots, (b + 1) * slots)):
                s3[j].start()

    for j in (7, 6, 5, 4):
        s3[8 + j].wait_recv()
        part[j] = (part[j].astype(F32) + r3[j].astype(F32)).astype(BF16)
        s2[j].start()
    for j in (3, 2):
        s3[8 + j].wait_recv()
        s2[4 + j].wait_recv()
        part[j] = (part[j].astype(F32) + r3[j].astype(F32) + r2[j].astype(F32)).astype(BF16)
        s1[j].start()

    def total_of(j):
        s3[8 + j].wait_recv()
        s2[4 + j].wait_recv()
        s1[2 + j].wait_recv()
        return part[j].astype(F32) + r3[j].astype(F32) + r2[j].astype(F32) + r1[j].astype(F32)

    part[1] = total_of(1).astype(BF16)
    s0.start()
    keep = total_of(0)
    s0.wait_recv()
    other = r0[...].astype(F32)
    gate_move = jnp.where(moved, mod_recv[2:3, :], mods[2, 1:2, :])
    upd_ref[0] = (stay_ref[...].astype(F32) + mods[2, 0:1, :] * jnp.where(is_a, keep, other)).astype(BF16)
    upd_ref[1] = (move_ref[...].astype(F32) + gate_move * jnp.where(is_a, other, keep)).astype(BF16)

    md.wait_send()
    t0.wait_send()
    for copy in z_copies + swaps + d1 + d2 + d3:
        copy.wait_send()
    for copy in [*s3.values(), *s2.values(), *s1.values(), s0]:
        copy.wait_send()


def body(latents, timestep, target, qkv_weight, mod_weight, out_weight):
    slots = latents.shape[1]
    tok = latents.shape[0]
    depth = latents.shape[2]
    home = lax.axis_index("section")
    prev = jnp.maximum(home - 1, 0)
    own_target = lax.dynamic_slice_in_dim(target, home * slots, slots)
    prev_target = lax.dynamic_slice_in_dim(target, prev * slots, slots)
    own_steps = lax.dynamic_slice_in_dim(timestep, home * slots, slots)
    prev_steps = lax.dynamic_slice_in_dim(timestep, prev * slots, slots)
    first_moves = own_target[0] != home
    moved = first_moves | (own_target[1] != home)
    prev_first = prev_target[0] != prev
    stay_step = jnp.where(first_moves, own_steps[1], own_steps[0])
    move_step = jnp.where(first_moves, own_steps[0], own_steps[1])
    prev_step = jnp.where(prev_first, prev_steps[0], prev_steps[1])
    lane = jnp.arange(8, dtype=jnp.int32)
    steps = jnp.where(lane == 0, stay_step, jnp.where(lane == 1, move_step, prev_step))
    feature = split_feature(steps)
    stay = jnp.where(first_moves, latents[:, 1], latents[:, 0])
    move = jnp.where(first_moves, latents[:, 0], latents[:, 1])
    mod_table = jnp.transpose(mod_weight[0], (1, 0, 2))
    wqkv = jnp.transpose(qkv_weight[0], (1, 0, 2))
    wout = out_weight[0]
    vmem = pl.BlockSpec(memory_space=pltpu.VMEM)
    hbm = pl.BlockSpec(memory_space=pl.ANY)
    dma = pltpu.SemaphoreType.DMA
    updated = pl.pallas_call(
        kernel,
        out_shape=jax.ShapeDtypeStruct((2, tok, depth), BF16),
        in_specs=[pl.BlockSpec(memory_space=pltpu.SMEM), vmem, vmem, vmem, hbm, hbm, hbm],
        out_specs=vmem,
        scratch_shapes=[
            pltpu.VMEM(mod_table.shape, BF16),
            pltpu.VMEM((3, 8, depth), F32),
            pltpu.VMEM((8, depth), F32),
            pltpu.VMEM((8, depth), F32),
            pltpu.VMEM((tok, depth), BF16),
            pltpu.VMEM((16, tok, depth), BF16),
            pltpu.VMEM((3, depth, 2 * HEAD_DIM), BF16),
            pltpu.VMEM((2 * HEAD_DIM, depth), BF16),
            pltpu.VMEM((3, depth, HEAD_DIM), BF16),
            pltpu.VMEM((HEAD_DIM, depth), BF16),
            pltpu.VMEM((3, depth, HEAD_DIM), BF16),
            pltpu.VMEM((HEAD_DIM, depth), BF16),
            pltpu.VMEM((3, 16 * tok, 2 * HEAD_DIM), BF16),
            pltpu.VMEM((16, tok, depth), BF16),
            pltpu.VMEM((8, tok, depth), BF16),
            pltpu.VMEM((4, tok, depth), BF16),
            pltpu.VMEM((2, tok, depth), BF16),
            pltpu.VMEM((tok, depth), BF16),
            dma((5,)),
            dma,
            dma,
            dma((4,)),
            dma((4,)),
            dma((4,)),
            dma((4,)),
            dma((15,)),
            dma((15,)),
            dma((15,)),
            dma((15,)),
        ],
        compiler_params=pltpu.CompilerParams(
            collective_id=0, has_side_effects=True, vmem_limit_bytes=56 * 1024 * 1024
        ),
    )(moved.astype(jnp.int32)[None], feature, stay, move, mod_table, wqkv, wout)
    first = jnp.where(first_moves, updated[1], updated[0])
    second = jnp.where(first_moves, updated[0], updated[1])
    return jnp.stack([first, second], axis=1)


def solution(mesh):
    return jax.shard_map(
        body,
        mesh=mesh,
        in_specs=(
            P("tp", "section", None),
            P(),
            P(),
            P("section", None, None, "tp"),
            P("section", None, None, None),
            P("section", "tp", None),
        ),
        out_specs=P("tp", "section", None),
        check_vma=False,
    )
```

time: 259 us -> 102 us (0.39)
  the two profiles are of different devices: /device:TPU:1 before, /device:TPU:8 now
where the time goes in v1:
time: 102 us; the launch traced here: 99.9 us
  Pallas kernels  85.3 us (84%)
  local copies, waits for them, and re-layouts  6.27 us (6%)
  between operations  5.28 us (5%)
  other arithmetic  3.04 us (3%)
    pallas_call x1, Pallas kernels, body(): pl.pallas_call(kernel, out_shape=jax.ShapeDtypeStruct((2, tok, depth), BF...  85.3 us
    slice x1, local copies, waits for them, and re-layouts, body(): stay = jnp.where(first_moves, latents[:, 1], latents[:, 0])  2.22 us

profile of v1, /device:TPU:8, one launch (start us, length us, event | category | flops | bytes accessed | tf_op | source)
XLA Modules:
  0.0 99.9 jit_solution(4232216236765601022)
XLA Ops:
  0.0 0.1 pad.5.clone
  0.1 0.8 fusion.4
  1.0 0.7 fusion.3
  1.6 0.6 fusion.5
  3.5 0.6 fusion.7
  8.0 0.1 multiply_cosine_fusion
  8.1 0.7 maximum_maximum_fusion.feat_ref
  8.8 2.2 %fusion.2 = (bf16[64,1,2048]{2,1,0:T(2,128)(2,1)S(1)}, bf16[64,1,2048]{2,1,0:T(2,128)(2,1)S(1)}) fusion(bf16[64,2,2048]{2,1,0:T(2,128)(2,1)} %param.6), kind=kLoop, calls=%fused_computation.19 | loop fusion | bytes 1048576 | tf_op jit(solution)/shard_map/slice | solution.py:287
  11.0 1.1 %select_bitcast_fusion.2 = (bf16[64,2048]{1,0:T(8,128)(2,1)}, bf16[64,2048]{1,0:T(8,128)(2,1)}) fusion(pred[]{:T(512)S(6)} %ne.9, bf16[64,1,2048]{2,1,0:T(2,128)(2,1)S(1)} %get-tuple-element.10, bf16[64,1,2048]{2,1,0:T(2,128)(2,1)S(1)} %get-tuple-element.9), kind=kLoop, calls=%fused_computation.3 | loop fusion | flops 262144 | bytes 1048577 | tf_op jit(solution)/shard_map/jit(_where)/select_n | solution.py:288
  12.1 85.3 %shard_map.64 = bf16[2,64,2048]{2,1,0:T(8,128)(2,1)} custom-call(s32[1]{0:T(128)} %bitcast.2.flag_ref, bf16[32,256]{1,0:T(8,128)(2,1)} %maximum_maximum_fusion.feat_ref, bf16[64,2048]{1,0:T(8,128)(2,1)} %get-tuple-element.6.stay_ref, bf16[64,2048]{1,0:T(8,128)(2,1)} %get-tuple-element.5.move_ref, bf16[3,256,2048]{2,1,0:T(8,128)(2,1)} %bitcast.24, ...), custom_call_target="tpu_custom_call" | custom-call | tf_op jit(solution)/shard_map/pallas_call | solution.py:295
  97.4 1.1 %select_bitcast_fusion.1 = (bf16[64,1,2048]{2,0,1:T(8,128)(2,1)S(1)}, bf16[64,1,2048]{2,0,1:T(8,128)(2,1)S(1)}) fusion(pred[]{:T(512)S(6)} %ne.9, bf16[2,64,2048]{2,1,0:T(8,128)(2,1)} %shard_map.64), kind=kLoop, calls=%fused_computation.2 | loop fusion | flops 262144 | bytes 1048577 | tf_op jit(solution)/shard_map/jit(_where)/select_n | solution.py:335
  98.5 0.1 pad_maximum_fusion
  98.6 1.3 %copy.9 = bf16[64,2,2048]{2,1,0:T(2,128)(2,1)} copy(bf16[64,2,2048]{2,0,1:T(8,128)(2,1)S(1)} %pad_maximum_fusion) | data formatting | bytes 1048576 | tf_op jit(solution)/shard_map/stack | solution.py:337
  (4 shorter events, 0.0 us)

commit v2 on v1

--- a/solution.py
+++ b/solution.py
@@ -28,11 +28,11 @@
     rest = feature - high
     mid = lax.reduce_precision(rest, 8, 7)
     low = rest - mid
-    return jnp.concatenate([high, mid, low, jnp.zeros_like(low)], axis=0).astype(BF16)
+    return jnp.concatenate([high, mid, low], axis=0).astype(BF16)
 
 
 def kernel(
-    flag_ref, feat_ref, stay_ref, move_ref, mod_hbm, wqkv_hbm, wout_hbm,
+    target_ref, feat_ref, lat_ref, mod_hbm, wqkv_hbm, wout_hbm,
     upd_ref,
     mod_v, mods, mod_send, mod_recv, hid_send,
     gath, w2, wo2, wn, wno, ws, wso,
@@ -40,7 +40,8 @@
     ld_sem, md_s, md_r, z_s, z_r, sw_s, sw_r, tok_s, tok_r, rs_s, rs_r,
 ):
     sections = lax.axis_size("section")
-    tok = stay_ref.shape[0]
+    tok = lat_ref.shape[1]
+    latents = feat_ref.shape[0] // 3
     sec = lax.axis_index("section")
     tp = lax.axis_index("tp")
     core = lax.rem(sec, 2)
@@ -62,7 +63,10 @@
     before = (lax.rem(sec + sections - 1, sections), tp)
     after = (lax.rem(sec + 1, sections), tp)
     is_a = (u == 0) | (u == 3)
-    moved = flag_ref[0] != 0
+    prev = jnp.maximum(sec - 1, 0)
+    first_moves = target_ref[2 * sec] != sec
+    moved = first_moves | (target_ref[2 * sec + 1] != sec)
+    prev_first = target_ref[2 * prev] != prev
 
     def remote(src, dst, ssem, rsem, peer):
         return pltpu.make_async_remote_copy(
@@ -94,29 +98,39 @@
     mod_send[...] = jnp.zeros_like(mod_send)
     for c in range(3):
         prod = jnp.dot(feat_ref[...], mod_v[c], preferred_element_type=F32)
-        full = prod[0:8] + prod[8:16] + prod[16:24]
-        mods[c] = full
-        mod_send[pl.ds(c, 1), :] = full[2:3]
+        mods[c] = prod[0:latents] + prod[latents : 2 * latents] + prod[2 * latents : 3 * latents]
+        mod_send[pl.ds(c, 1), :] = jnp.where(
+            prev_first, mods[c, pl.ds(2 * prev, 1), :], mods[c, pl.ds(2 * prev + 1, 1), :]
+        )
     md = remote(mod_send, mod_recv, md_s, md_r, before)
     md.start()
     for copy in z_copies:
         copy.start()
 
-    def norm(ref, shift, scale):
-        values = ref[...].astype(F32)
+    def mod_row(c, moving):
+        first = mods[c, pl.ds(2 * sec, 1), :]
+        second = mods[c, pl.ds(2 * sec + 1, 1), :]
+        if moving:
+            return jnp.where(moved, mod_recv[pl.ds(c, 1), :], jnp.where(first_moves, first, second))
+        return jnp.where(first_moves, second, first)
+
+    def tokens(moving):
+        if moving:
+            return jnp.where(first_moves, lat_ref[0], lat_ref[1]).astype(F32)
+        return jnp.where(first_moves, lat_ref[1], lat_ref[0]).astype(F32)
+
+    def norm(moving):
+        values = tokens(moving)
+        shift, scale = mod_row(0, moving), mod_row(1, moving)
         centred = values - jnp.mean(values, axis=-1, keepdims=True)
         variance = jnp.mean(centred * centred, axis=-1, keepdims=True)
         return (centred * lax.rsqrt(variance + 1e-06) * (1.0 + scale) + shift).astype(BF16)
 
-    stay_hidden = norm(stay_ref, mods[0, 0:1, :], mods[1, 0:1, :])
+    stay_hidden = norm(False)
     gath[0] = stay_hidden
     hid_send[...] = stay_hidden
     md.wait_recv()
-    move_hidden = norm(
-        move_ref,
-        jnp.where(moved, mod_recv[0:1, :], mods[0, 1:2, :]),
-        jnp.where(moved, mod_recv[1:2, :], mods[1, 1:2, :]),
-    )
+    move_hidden = norm(True)
     gath[0] = jnp.where(is_a, gath[0], move_hidden)
     hid_send[...] = jnp.where(is_a, move_hidden, hid_send[...])
 
@@ -253,9 +267,10 @@
     keep = total_of(0)
     s0.wait_recv()
     other = r0[...].astype(F32)
-    gate_move = jnp.where(moved, mod_recv[2:3, :], mods[2, 1:2, :])
-    upd_ref[0] = (stay_ref[...].astype(F32) + mods[2, 0:1, :] * jnp.where(is_a, keep, other)).astype(BF16)
-    upd_ref[1] = (move_ref[...].astype(F32) + gate_move * jnp.where(is_a, other, keep)).astype(BF16)
+    stay_out = (tokens(False) + mod_row(2, False) * jnp.where(is_a, keep, other)).astype(BF16)
+    move_out = (tokens(True) + mod_row(2, True) * jnp.where(is_a, other, keep)).astype(BF16)
+    upd_ref[0] = jnp.where(first_moves, move_out, stay_out)
+    upd_ref[1] = jnp.where(first_moves, stay_out, move_out)
 
     md.wait_send()
     t0.wait_send()
@@ -266,26 +281,9 @@
 
 
 def body(latents, timestep, target, qkv_weight, mod_weight, out_weight):
-    slots = latents.shape[1]
     tok = latents.shape[0]
     depth = latents.shape[2]
-    home = lax.axis_index("section")
-    prev = jnp.maximum(home - 1, 0)
-    own_target = lax.dynamic_slice_in_dim(target, home * slots, slots)
-    prev_target = lax.dynamic_slice_in_dim(target, prev * slots, slots)
-    own_steps = lax.dynamic_slice_in_dim(timestep, home * slots, slots)
-    prev_steps = lax.dynamic_slice_in_dim(timestep, prev * slots, slots)
-    first_moves = own_target[0] != home
-    moved = first_moves | (own_target[1] != home)
-    prev_first = prev_target[0] != prev
-    stay_step = jnp.where(first_moves, own_steps[1], own_steps[0])
-    move_step = jnp.where(first_moves, own_steps[0], own_steps[1])
-    prev_step = jnp.where(prev_first, prev_steps[0], prev_steps[1])
-    lane = jnp.arange(8, dtype=jnp.int32)
-    steps = jnp.where(lane == 0, stay_step, jnp.where(lane == 1, move_step, prev_step))
-    feature = split_feature(steps)
-    stay = jnp.where(first_moves, latents[:, 1], latents[:, 0])
-    move = jnp.where(first_moves, latents[:, 0], latents[:, 1])
+    feature = split_feature(timestep)
     mod_table = jnp.transpose(mod_weight[0], (1, 0, 2))
     wqkv = jnp.transpose(qkv_weight[0], (1, 0, 2))
     wout = out_weight[0]
@@ -295,11 +293,11 @@
     updated = pl.pallas_call(
         kernel,
         out_shape=jax.ShapeDtypeStruct((2, tok, depth), BF16),
-        in_specs=[pl.BlockSpec(memory_space=pltpu.SMEM), vmem, vmem, vmem, hbm, hbm, hbm],
+        in_specs=[pl.BlockSpec(memory_space=pltpu.SMEM), vmem, vmem, hbm, hbm, hbm],
         out_specs=vmem,
         scratch_shapes=[
             pltpu.VMEM(mod_table.shape, BF16),
-            pltpu.VMEM((3, 8, depth), F32),
+            pltpu.VMEM((3, timestep.shape[0], depth), F32),
             pltpu.VMEM((8, depth), F32),
             pltpu.VMEM((8, depth), F32),
             pltpu.VMEM((tok, depth), BF16),
@@ -331,10 +329,8 @@
         compiler_params=pltpu.CompilerParams(
             collective_id=0, has_side_effects=True, vmem_limit_bytes=56 * 1024 * 1024
         ),
-    )(moved.astype(jnp.int32)[None], feature, stay, move, mod_table, wqkv, wout)
-    first = jnp.where(first_moves, updated[1], updated[0])
-    second = jnp.where(first_moves, updated[0], updated[1])
-    return jnp.stack([first, second], axis=1)
+    )(target, feature, jnp.transpose(latents, (1, 0, 2)), mod_table, wqkv, wout)
+    return jnp.transpose(updated, (1, 0, 2))
 
 
 def solution(mesh):

time: 102 us -> 93.1 us (0.913)
  between operations: 5.28 us -> 0.03 us
  local copies, waits for them, and re-layouts: 6.27 us -> 4.37 us
  other arithmetic: 3.04 us -> 1.41 us
    slice x4 -> x0, local copies, waits for them, and re-layouts: 4.04 us -> none  [the longest x1 2.22 us: body(): stay = jnp.where(first_moves, latents[:, 1], latents[:, 0])]
    transpose x0 -> x1, local copies, waits for them, and re-layouts: none -> 2.37 us  [body(): return jnp.transpose(updated, (1, 0, 2))]
    select_n x2 -> x0, other arithmetic: 2.16 us -> none  [the longest x1 1.09 us: body(): move = jnp.where(first_moves, latents[:, 0], latents[:, 1])]
    unnamed x0 -> x1, local copies, waits for them, and re-layouts: none -> 1.99 us
    another operation x1 -> x0, local copies, waits for them, and re-layouts: 1.33 us -> none  [body(): return jnp.stack([first, second], axis=1)]
where the time goes in v2:
time: 93.1 us; the launch traced here: 91.3 us
  Pallas kernels  85.5 us (92%)
  local copies, waits for them, and re-layouts  4.37 us (5%)
  other arithmetic  1.41 us (2%)
    pallas_call x1, Pallas kernels, body(): pl.pallas_call(kernel, out_shape=jax.ShapeDtypeStruct((2, tok, depth), BF...  85.5 us
    transpose x1, local copies, waits for them, and re-layouts, body(): return jnp.transpose(updated, (1, 0, 2))  2.37 us
    unnamed x1, local copies, waits for them, and re-layouts  1.99 us

profile of v2, /device:TPU:8, one launch (start us, length us, event | category | flops | bytes accessed | tf_op | source)
XLA Modules:
  0.0 91.3 jit_solution(13267621312052124709)
XLA Ops:
  0.0 0.7 convert_element_type.4
  0.7 0.1 multiply_cosine_fusion
  0.8 0.6 pad_maximum_fusion.feat_ref
  1.4 2.0 %copy.10 = bf16[64,2,2048]{2,0,1:T(8,128)(2,1)} copy(bf16[64,2,2048]{2,1,0:T(2,128)(2,1)} %param.6) | data formatting | bytes 1048576 | tf_op args[0]
  3.4 85.5 %shard_map.64 = bf16[2,64,2048]{2,1,0:T(8,128)(2,1)} custom-call(s32[16]{0:T(128)} %target_ref.1, bf16[48,256]{1,0:T(8,128)(2,1)} %pad_maximum_fusion.feat_ref, bf16[2,64,2048]{2,1,0:T(8,128)(2,1)} %bitcast.13, bf16[3,256,2048]{2,1,0:T(8,128)(2,1)} %bitcast.11, bf16[3,2048,128]{2,1,0:T(8,128)(2,1)} %bitcast.14, bf16[128,2048]{1,0:T(8,128)(2,1)} %bitcast.15), custom_call_target="tpu_custom_call" | custom-call | tf_op jit(solution)/shard_map/pallas_call | solution.py:293
  89.0 2.4 %copy.8 = bf16[64,2,2048]{2,1,0:T(2,128)(2,1)} copy(bf16[64,2,2048]{2,0,1:T(8,128)(2,1)} %bitcast.12) | data formatting | bytes 1048576 | tf_op jit(solution)/shard_map/transpose | solution.py:333
  (2 shorter events, 0.0 us)

commit v3 on v2

v3 whole, which is shorter than its diff:
```python
import functools
import math

import jax
import jax.numpy as jnp
from jax import lax
from jax.experimental import pallas as pl
from jax.experimental.pallas import tpu as pltpu
from jax.sharding import PartitionSpec as P

HEAD_DIM = 128
FREQ = 256
MESH = pl.DeviceIdType.MESH
BF16 = jnp.bfloat16
F32 = jnp.float32


def time_embed(steps):
    half_width = FREQ // 2
    frequency = jnp.exp(-math.log(10000.0) * jnp.arange(half_width, dtype=F32) / half_width)
    angles = steps.astype(F32)[:, None] * frequency[None, :]
    return jnp.concatenate([jnp.cos(angles), jnp.sin(angles)], axis=1)


def split_feature(steps):
    feature = jax.nn.silu(time_embed(steps))
    high = lax.reduce_precision(feature, 8, 7)
    rest = feature - high
    mid = lax.reduce_precision(rest, 8, 7)
    low = rest - mid
    return jnp.concatenate([high, mid, low], axis=0).astype(BF16)


def kernel(
    target_ref, feat_ref, lat_ref, mod_hbm, wqkv_hbm, wout_hbm,
    upd_ref,
    mod_v, mods, mod_send, mod_recv, hid_send,
    gath, w2, wo2, wn, wno, ws, wso,
    qkv, part, rf, rg, r1, r0,
    ld_sem, md_s, md_r, z_s, z_r, sw_s, sw_r, tok_s, tok_r, rs_s, rs_r,
):
    sections = lax.axis_size("section")
    tok = lat_ref.shape[1]
    depth = lat_ref.shape[2]
    latents = feat_ref.shape[0] // 3
    sec = lax.axis_index("section")
    tp = lax.axis_index("tp")
    core = lax.rem(sec, 2)
    x = tp // 4
    y = lax.rem(tp, 4)
    u = jnp.where(core == 0, y, x)
    v = jnp.where(core == 0, x, y)

    def at(uu, vv):
        return jnp.where(core == 0, vv * 4 + uu, uu * 4 + vv)

    def flip(a):
        return a + 1 - 2 * lax.rem(a, 2)

    pair = (sec, at(flip(u), v))
    p1 = (sec, at(3 - u, v))
    p2 = (sec, at(u, flip(v)))
    p3 = (sec, at(u, 3 - v))
    before = (lax.rem(sec + sections - 1, sections), tp)
    after = (lax.rem(sec + 1, sections), tp)
    is_a = (u == 0) | (u == 3)
    is_b = jnp.logical_not(is_a)
    prev = jnp.maximum(sec - 1, 0)
    first_moves = target_ref[2 * sec] != sec
    moved = first_moves | (target_ref[2 * sec + 1] != sec)
    prev_first = target_ref[2 * prev] != prev

    def remote(src, dst, ssem, rsem, peer):
        return pltpu.make_async_remote_copy(
            src_ref=src, dst_ref=dst, send_sem=ssem, recv_sem=rsem,
            device_id=peer, device_id_type=MESH,
        )

    own_lanes = pl.ds(0, HEAD_DIM)
    pair_lanes = pl.ds(HEAD_DIM, HEAD_DIM)
    mod_loads = [pltpu.make_async_copy(mod_hbm.at[c], mod_v.at[c], ld_sem.at[4 + c]) for c in range(3)]
    for load in mod_loads:
        load.start()

    barrier = pltpu.get_barrier_semaphore()
    for peer in (pair, p1, p2, p3, before, after):
        pl.semaphore_signal(barrier, inc=1, device_id=peer, device_id_type=MESH)
    pl.semaphore_wait(barrier, 6)

    z_copies = [
        remote(wqkv_hbm.at[i], wn.at[i], z_s.at[i], z_r.at[i], before) for i in range(1, 3)
    ]
    z_copies.append(remote(wout_hbm, wno, z_s.at[3], z_r.at[3], before))
    rows_half = wn.shape[1] // 2
    z_first = [
        remote(wqkv_hbm.at[0, rs], wn.at[0, rs], z_s.at[4 * k], z_r.at[4 * k], before)
        for k, rs in enumerate((pl.ds(0, rows_half), pl.ds(rows_half, rows_half)))
    ]

    def next_arrived(i):
        for copy in z_first if i == 0 else z_copies[i - 1 : i]:
            copy.wait_recv()

    direct = [
        remote(wqkv_hbm.at[i], w2.at[i, :, pair_lanes], sw_s.at[i], sw_r.at[i], pair)
        for i in range(3)
    ]
    direct.append(remote(wout_hbm, wo2.at[pair_lanes], sw_s.at[3], sw_r.at[3], pair))
    chosen = [
        remote(ws.at[i], w2.at[i, :, pair_lanes], sw_s.at[i], sw_r.at[i], pair)
        for i in range(3)
    ]
    chosen.append(remote(wso, wo2.at[pair_lanes], sw_s.at[3], sw_r.at[3], pair))
    z_first[0].start()

    @pl.when(is_b)
    def _():
        direct[0].start()

    loads = [
        pltpu.make_async_copy(wqkv_hbm.at[i], w2.at[i, :, own_lanes], ld_sem.at[i])
        for i in range(3)
    ]
    loads.append(pltpu.make_async_copy(wout_hbm, wo2.at[own_lanes], ld_sem.at[3]))
    loads[0].start()

    def select_weight(i, take_next, in_place):
        if i < 3:
            rows = w2.shape[1]
            step = min(512, rows)

            def piece(b, carry):
                rs = pl.ds(pl.multiple_of(b * step, step), step)
                picked = jnp.where(take_next, wn[i, rs, :], w2[i, rs, own_lanes])
                if in_place:
                    w2[i, rs, own_lanes] = picked
                else:
                    ws[i, rs, :] = picked
                return carry

            lax.fori_loop(0, rows // step, piece, 0)
        else:
            picked = jnp.where(take_next, wno[...], wo2[own_lanes, :])
            if in_place:
                wo2[own_lanes, :] = picked
            else:
                wso[...] = picked

    def send_weight(i, which):
        @pl.when(is_a & (core == which))
        def _():
            loads[i].wait()
            next_arrived(i)
            select_weight(i, moved, False)
            chosen[i].start()

    def make_mods(c):
        mod_loads[c].wait()
        prod = jnp.dot(feat_ref[...], mod_v[c], preferred_element_type=F32)
        mods[c] = prod[0:latents] + prod[latents : 2 * latents] + prod[2 * latents : 3 * latents]
        mod_send[c // 2, pl.ds(c % 2, 1), :] = jnp.where(
            prev_first, mods[c, pl.ds(2 * prev, 1), :], mods[c, pl.ds(2 * prev + 1, 1), :]
        )

    mod_send[...] = jnp.zeros_like(mod_send)
    md = [remote(mod_send.at[k], mod_recv.at[k], md_s.at[k], md_r.at[k], before) for k in range(2)]
    make_mods(0)
    make_mods(1)
    md[0].start()
    z_first[1].start()
    for copy in z_copies:
        copy.start()
    for load in loads[1:]:
        load.start()

    def mod_row(c, moving):
        first = mods[c, pl.ds(2 * sec, 1), :]
        second = mods[c, pl.ds(2 * sec + 1, 1), :]
        if moving:
            arrived = mod_recv[c // 2, pl.ds(c % 2, 1), :]
            return jnp.where(moved, arrived, jnp.where(first_moves, first, second))
        return jnp.where(first_moves, second, first)

    def tokens(moving):
        if moving:
            return jnp.where(first_moves, lat_ref[0], lat_ref[1]).astype(F32)
        return jnp.where(first_moves, lat_ref[1], lat_ref[0]).astype(F32)

    def centre(moving):
        values = tokens(moving)
        centred = values - jnp.mean(values, axis=-1, keepdims=True)
        variance = jnp.mean(centred * centred, axis=-1, keepdims=True)
        return centred * lax.rsqrt(variance + 1e-06)

    def modulate(normed, moving):
        return (normed * (1.0 + mod_row(1, moving)) + mod_row(0, moving)).astype(BF16)

    cuts = 2
    piece_rows = tok // cuts

    def place(p):
        return gath.at[p // cuts, pl.ds((p % cuts) * piece_rows, piece_rows)]

    def doubling(slots_before, peer):
        count, first_sem = slots_before * cuts, (slots_before - 1) * cuts
        return [
            remote(place(p), place(count + p), tok_s.at[first_sem + p], tok_r.at[first_sem + p], peer)
            for p in range(count)
        ]

    t0 = [
        remote(hid_send.at[pl.ds(p * piece_rows, piece_rows)], place(cuts + p), tok_s.at[p], tok_r.at[p], pair)
        for p in range(cuts)
    ]
    d1, d2, d3 = doubling(2, p1), doubling(4, p2), doubling(8, p3)

    def pass_on(p):
        d3[p].start()
        if p < 4 * cuts:
            d2[p].start()
        if p < 2 * cuts:
            d1[p].start()

    stay_hidden = modulate(centre(False), False)

    @pl.when(is_a)
    def _():
        gath[0] = stay_hidden
        for p in range(cuts):
            pass_on(p)

    @pl.when(is_b)
    def _():
        hid_send[...] = stay_hidden
        for copy in t0:
            copy.start()

    send_weight(0, 0)
    md[0].wait_recv()
    move_hidden = modulate(centre(True), True)

    @pl.when(is_a)
    def _():
        hid_send[...] = move_hidden
        for copy in t0:
            copy.start()

    @pl.when(is_b)
    def _():
        gath[0] = move_hidden
        for p in range(cuts):
            pass_on(p)
        for i in range(1, 4):
            direct[i].start()

    make_mods(2)
    md[1].start()
    send_weight(1, 0)
    send_weight(0, 1)
    for p in range(cuts):
        t0[p].wait_recv()
        pass_on(cuts + p)
    send_weight(2, 0)
    for p in range(2 * cuts):
        d1[p].wait_recv()
        pass_on(2 * cuts + p)
    send_weight(3, 0)
    send_weight(1, 1)
    for p in range(2 * cuts):
        d2[p].wait_recv()
        pass_on(4 * cuts + p)
    send_weight(2, 1)
    for p in range(2 * cuts, 4 * cuts):
        d2[p].wait_recv()
        pass_on(4 * cuts + p)
    send_weight(3, 1)

    slots = 4
    width = slots * tok

    @pl.when(is_b)
    def _():
        for i in range(4):
            loads[i].wait()
            next_arrived(i)
            select_weight(i, moved, True)

    def project(i, b):
        rows = gath[pl.ds(b * slots, slots)].reshape(width, depth)
        out = jnp.dot(rows, w2[i], preferred_element_type=F32)
        qkv[i, pl.ds(b * width, width), :] = out.astype(BF16)

    for i in range(3):
        chosen[i].wait_recv()
        project(i, 0)
        project(i, 1)
    for b in (2, 3):
        for p in range(4 * cuts):
            d3[4 * cuts * (b - 2) + p].wait_recv()
        for i in range(3):
            project(i, b)
    chosen[3].wait_recv()

    half = depth // 2
    lanes_of = [pl.ds(0, half), pl.ds(half, half)]

    def low(j):
        return j if j < 4 else j - 4

    first, second, third, fourth = [{}, {}], [{}, {}], [{}, {}], []
    for h in range(2):
        lanes = lanes_of[h]
        jump = 8 - 4 * h
        goals = range(8) if h == 0 else (0, 1, 2, 3, 8, 9, 10, 11)

        def hop(src, dst, sem, peer):
            return remote(src, dst, rs_s.at[15 * h + sem], rs_r.at[15 * h + sem], peer)

        for n, j in enumerate(goals):
            first[h][j] = hop(part.at[j + jump, :, lanes], rf.at[h, n], n, (p3, p2)[h])
        for j in range(4):
            second[h][j] = hop(part.at[j + 12 - jump, :, lanes], rg.at[h, j], 8 + j, (p2, p3)[h])
        for j in range(2):
            third[h][j] = hop(part.at[j + 2, :, lanes], r1.at[j, :, lanes], 12 + j, p1)
        fourth.append(hop(part.at[1, :, lanes], r0.at[:, lanes], 14, pair))

    factor = HEAD_DIM ** (-0.5) * math.log2(math.e)
    n_col = 4
    col = depth // n_col

    def attend(b):
        rows = pl.ds(b * width, width)
        heads = []
        for h in range(2):
            lanes = pl.ds(h * HEAD_DIM, HEAD_DIM)
            scores = lax.dot_general(
                qkv[0, rows, lanes], qkv[1, :, lanes], (((1,), (1,)), ((), ())),
                preferred_element_type=F32,
            )
            top = jnp.max(scores, axis=-1, keepdims=True)
            weights = jnp.exp2((scores - top) * factor)
            total = jnp.sum(weights, axis=-1, keepdims=True)
            mixed = jnp.dot(weights.astype(BF16), qkv[2, :, lanes], preferred_element_type=F32)
            heads.append((mixed / total).astype(BF16))
        both = jnp.concatenate(heads, axis=1)
        for n in range(n_col):
            lanes = pl.ds(n * col, col)
            out = jnp.dot(both, wo2[:, lanes], preferred_element_type=F32).astype(BF16)
            part[pl.ds(b * slots, slots), :, lanes] = out.reshape(slots, tok, col)

    def begin(*goals):
        for h, j in goals:
            first[h][j].start()

    def second_stage(k):
        for h in range(2):
            j = k + 4 + 4 * h
            first[h][j].wait_recv()
            arrived = rf[h, j - 4 * h].astype(F32)
            part[j, :, lanes_of[h]] = (part[j, :, lanes_of[h]].astype(F32) + arrived).astype(BF16)
            second[h][k].start()

    def settle(k, h):
        first[h][k].wait_recv()
        second[h][k].wait_recv()
        own = part[k, :, lanes_of[h]].astype(F32)
        return own + rf[h, k].astype(F32) + rg[h, k].astype(F32)

    def third_stage(k):
        for h in range(2):
            part[k, :, lanes_of[h]] = settle(k, h).astype(BF16)
            third[h][k - 2].start()

    def finish(k, h):
        total = settle(k, h)
        third[h][k].wait_recv()
        return total + r1[k, :, lanes_of[h]].astype(F32)

    attend(3)
    begin((0, 7), (1, 11), (0, 5), (1, 9))
    attend(2)
    begin((0, 3), (0, 1))
    attend(1)
    begin((1, 3), (1, 1))
    attend(0)
    second_stage(3)
    second_stage(1)
    begin((0, 6), (1, 10), (0, 2), (1, 2), (0, 4), (1, 8), (0, 0), (1, 0))
    third_stage(3)
    second_stage(2)
    second_stage(0)
    for h in range(2):
        part[1, :, lanes_of[h]] = finish(1, h).astype(BF16)
        fourth[h].start()
    third_stage(2)
    keep = jnp.concatenate([finish(0, 0), finish(0, 1)], axis=1)
    md[1].wait_recv()
    for copy in fourth:
        copy.wait_recv()
    other = r0[...].astype(F32)
    stay_out = (tokens(False) + mod_row(2, False) * jnp.where(is_a, keep, other)).astype(BF16)
    move_out = (tokens(True) + mod_row(2, True) * jnp.where(is_a, other, keep)).astype(BF16)
    upd_ref[0] = jnp.where(first_moves, move_out, stay_out)
    upd_ref[1] = jnp.where(first_moves, stay_out, move_out)

    for copy in [*md, *z_first, *z_copies, *chosen, *t0, *d1, *d2, *d3, *fourth]:
        copy.wait_send()
    for group in (*first, *second, *third):
        for copy in group.values():
            copy.wait_send()


def body(latents, timestep, target, qkv_weight, mod_weight, out_weight):
    tok = latents.shape[0]
    depth = latents.shape[2]
    feature = split_feature(timestep)
    mod_table = jnp.transpose(mod_weight[0], (1, 0, 2))
    wqkv = jnp.transpose(qkv_weight[0], (1, 0, 2))
    wout = out_weight[0]
    vmem = pl.BlockSpec(memory_space=pltpu.VMEM)
    hbm = pl.BlockSpec(memory_space=pl.ANY)
    dma = pltpu.SemaphoreType.DMA
    updated = pl.pallas_call(
        kernel,
        out_shape=jax.ShapeDtypeStruct((2, tok, depth), BF16),
        in_specs=[pl.BlockSpec(memory_space=pltpu.SMEM), vmem, vmem, hbm, hbm, hbm],
        out_specs=vmem,
        scratch_shapes=[
            pltpu.VMEM(mod_table.shape, BF16),
            pltpu.VMEM((3, timestep.shape[0], depth), F32),
            pltpu.VMEM((2, 8, depth), F32),
            pltpu.VMEM((2, 8, depth), F32),
            pltpu.VMEM((tok, depth), BF16),
            pltpu.VMEM((16, tok, depth), BF16),
            pltpu.VMEM((3, depth, 2 * HEAD_DIM), BF16),
            pltpu.VMEM((2 * HEAD_DIM, depth), BF16),
            pltpu.VMEM((3, depth, HEAD_DIM), BF16),
            pltpu.VMEM((HEAD_DIM, depth), BF16),
            pltpu.VMEM((3, depth, HEAD_DIM), BF16),
            pltpu.VMEM((HEAD_DIM, depth), BF16),
            pltpu.VMEM((3, 16 * tok, 2 * HEAD_DIM), BF16),
            pltpu.VMEM((16, tok, depth), BF16),
            pltpu.VMEM((2, 8, tok, depth // 2), BF16),
            pltpu.VMEM((2, 4, tok, depth // 2), BF16),
            pltpu.VMEM((2, tok, depth), BF16),
            pltpu.VMEM((tok, depth), BF16),
            dma((7,)),
            dma((2,)),
            dma((2,)),
            dma((5,)),
            dma((5,)),
            dma((4,)),
            dma((4,)),
            dma((30,)),
            dma((30,)),
            dma((30,)),
            dma((30,)),
        ],
        compiler_params=pltpu.CompilerParams(
            collective_id=0, has_side_effects=True, vmem_limit_bytes=54 * 1024 * 1024
        ),
    )(target, feature, jnp.transpose(latents, (1, 0, 2)), mod_table, wqkv, wout)
    return jnp.transpose(updated, (1, 0, 2))


def solution(mesh):
    return jax.shard_map(
        body,
        mesh=mesh,
        in_specs=(
            P("tp", "section", None),
            P(),
            P(),
            P("section", None, None, "tp"),
            P("section", None, None, None),
            P("section", "tp", None),
        ),
        out_specs=P("tp", "section", None),
        check_vma=False,
    )
```

time: 93.1 us -> 84.7 us (0.910)
  Pallas kernels: 85.5 us -> 77.8 us
    pallas_call x1, Pallas kernels: 85.5 us -> 77.8 us  [body(): pl.pallas_call(kernel, out_shape=jax.ShapeDtypeStruct((2, tok, depth), BF...]
where the time goes in v3:
time: 84.7 us; the launch traced here: 83.6 us
  Pallas kernels  77.8 us (92%)
  local copies, waits for them, and re-layouts  4.37 us (5%)
  other arithmetic  1.41 us (2%)
    pallas_call x1, Pallas kernels, body(): pl.pallas_call(kernel, out_shape=jax.ShapeDtypeStruct((2, tok, depth), BF...  77.8 us
    transpose x1, local copies, waits for them, and re-layouts, body(): return jnp.transpose(updated, (1, 0, 2))  2.37 us
    unnamed x1, local copies, waits for them, and re-layouts  1.99 us

profile of v3, /device:TPU:8, one launch (start us, length us, event | category | flops | bytes accessed | tf_op | source)
XLA Modules:
  0.0 83.6 jit_solution(14467725211935719427)
XLA Ops:
  0.0 0.7 convert_element_type.4
  0.7 0.1 multiply_cosine_fusion
  0.8 0.6 pad_maximum_fusion.feat_ref
  1.4 2.0 %copy.10 = bf16[64,2,2048]{2,0,1:T(8,128)(2,1)} copy(bf16[64,2,2048]{2,1,0:T(2,128)(2,1)} %param.6) | data formatting | bytes 1048576 | tf_op args[0]
  3.4 77.8 %shard_map.64 = bf16[2,64,2048]{2,1,0:T(8,128)(2,1)} custom-call(s32[16]{0:T(128)} %target_ref.1, bf16[48,256]{1,0:T(8,128)(2,1)} %pad_maximum_fusion.feat_ref, bf16[2,64,2048]{2,1,0:T(8,128)(2,1)} %bitcast.13, bf16[3,256,2048]{2,1,0:T(8,128)(2,1)} %bitcast.11, bf16[3,2048,128]{2,1,0:T(8,128)(2,1)} %bitcast.14, bf16[128,2048]{1,0:T(8,128)(2,1)} %bitcast.15), custom_call_target="tpu_custom_call" | custom-call | tf_op jit(solution)/shard_map/pallas_call | solution.py:423
  81.2 2.4 %copy.8 = bf16[64,2,2048]{2,1,0:T(2,128)(2,1)} copy(bf16[64,2,2048]{2,0,1:T(8,128)(2,1)} %bitcast.12) | data formatting | bytes 1048576 | tf_op jit(solution)/shard_map/transpose | solution.py:463
  (2 shorter events, 0.0 us)

commit v4 on v3

--- a/solution.py
+++ b/solution.py
@@ -32,9 +32,9 @@
 
 
 def kernel(
-    target_ref, feat_ref, lat_ref, mod_hbm, wqkv_hbm, wout_hbm,
+    target_ref, feat_ref, pairs_ref, mod_hbm, wqkv_hbm, wout_hbm,
     upd_ref,
-    mod_v, mods, mod_send, mod_recv, hid_send,
+    lat_ref, mod_v, mods, mod_send, mod_recv, hid_send,
     gath, w2, wo2, wn, wno, ws, wso,
     qkv, part, rf, rg, r1, r0,
     ld_sem, md_s, md_r, z_s, z_r, sw_s, sw_r, tok_s, tok_r, rs_s, rs_r,
@@ -172,6 +172,8 @@
         copy.start()
     for load in loads[1:]:
         load.start()
+    for k in range(2):
+        lat_ref[k] = pairs_ref[:, k, :]
 
     def mod_row(c, moving):
         first = mods[c, pl.ds(2 * sec, 1), :]
@@ -426,6 +428,7 @@
         in_specs=[pl.BlockSpec(memory_space=pltpu.SMEM), vmem, vmem, hbm, hbm, hbm],
         out_specs=vmem,
         scratch_shapes=[
+            pltpu.VMEM((2, tok, depth), BF16),
             pltpu.VMEM(mod_table.shape, BF16),
             pltpu.VMEM((3, timestep.shape[0], depth), F32),
             pltpu.VMEM((2, 8, depth), F32),
@@ -459,7 +462,7 @@
         compiler_params=pltpu.CompilerParams(
             collective_id=0, has_side_effects=True, vmem_limit_bytes=54 * 1024 * 1024
         ),
-    )(target, feature, jnp.transpose(latents, (1, 0, 2)), mod_table, wqkv, wout)
+    )(target, feature, latents, mod_table, wqkv, wout)
     return jnp.transpose(updated, (1, 0, 2))
 
 

time: 84.7 us -> 83.9 us (level); the launches traced: 83.6 us -> 83.7 us
  Pallas kernels: 77.8 us -> 79.9 us
  local copies, waits for them, and re-layouts: 4.37 us -> 2.37 us
    pallas_call x1, Pallas kernels: 77.8 us -> 79.9 us  [body(): pl.pallas_call(kernel, out_shape=jax.ShapeDtypeStruct((2, tok, depth), BF...]
    unnamed x1 -> x0, local copies, waits for them, and re-layouts: 1.99 us -> none
where the time goes in v4:
time: 83.9 us; the launch traced here: 83.7 us
  Pallas kernels  79.9 us (95%)
  local copies, waits for them, and re-layouts  2.37 us (3%)
  other arithmetic  1.42 us (2%)
    pallas_call x1, Pallas kernels, body(): pl.pallas_call(kernel, out_shape=jax.ShapeDtypeStruct((2, tok, depth), BF...  79.9 us
    transpose x1, local copies, waits for them, and re-layouts, body(): return jnp.transpose(updated, (1, 0, 2))  2.37 us

profile of v4, /device:TPU:8, one launch (start us, length us, event | category | flops | bytes accessed | tf_op | source)
XLA Modules:
  0.0 83.7 jit_solution(10604783441165273765)
XLA Ops:
  0.0 0.7 convert_element_type.4
  0.7 0.1 multiply_cosine_fusion
  0.8 0.6 pad_maximum_fusion.feat_ref
  1.4 79.9 %shard_map.64 = bf16[2,64,2048]{2,1,0:T(8,128)(2,1)} custom-call(s32[16]{0:T(128)} %target_ref.1, bf16[48,256]{1,0:T(8,128)(2,1)} %pad_maximum_fusion.feat_ref, bf16[64,2,2048]{2,1,0:T(2,128)(2,1)} %pairs_ref.1, bf16[3,256,2048]{2,1,0:T(8,128)(2,1)} %bitcast.8, bf16[3,2048,128]{2,1,0:T(8,128)(2,1)} %bitcast.10, bf16[128,2048]{1,0:T(8,128)(2,1)} %bitcast.11), custom_call_target="tpu_custom_call" | custom-call | tf_op jit(solution)/shard_map/pallas_call | solution.py:425
  81.3 2.4 %copy.7 = bf16[64,2,2048]{2,1,0:T(2,128)(2,1)} copy(bf16[64,2,2048]{2,0,1:T(8,128)(2,1)} %bitcast.9) | data formatting | bytes 1048576 | tf_op jit(solution)/shard_map/transpose | solution.py:466
  (2 shorter events, 0.0 us)

commit v5 on v4

--- a/solution.py
+++ b/solution.py
@@ -197,7 +197,7 @@
     def modulate(normed, moving):
         return (normed * (1.0 + mod_row(1, moving)) + mod_row(0, moving)).astype(BF16)
 
-    cuts = 2
+    cuts = 4
     piece_rows = tok // cuts
 
     def place(p):
@@ -454,8 +454,8 @@
             dma((5,)),
             dma((4,)),
             dma((4,)),
-            dma((30,)),
-            dma((30,)),
+            dma((60,)),
+            dma((60,)),
             dma((30,)),
             dma((30,)),
         ],

time: 83.9 us -> 83.4 us (level)
  no operation moved by 1% of the time
where the time goes in v5:
time: 83.4 us; the launch traced here: 83 us
  Pallas kernels  79.2 us (95%)
  local copies, waits for them, and re-layouts  2.37 us (3%)
  other arithmetic  1.42 us (2%)
    pallas_call x1, Pallas kernels, body(): pl.pallas_call(kernel, out_shape=jax.ShapeDtypeStruct((2, tok, depth), BF...  79.2 us
    transpose x1, local copies, waits for them, and re-layouts, body(): return jnp.transpose(updated, (1, 0, 2))  2.37 us

profile of v5, /device:TPU:8, one launch (start us, length us, event | category | flops | bytes accessed | tf_op | source)
XLA Modules:
  0.0 83.0 jit_solution(1166265951967370376)
XLA Ops:
  0.0 0.7 convert_element_type.4
  0.7 0.1 multiply_cosine_fusion
  0.8 0.6 pad_maximum_fusion.feat_ref
  1.4 79.2 %shard_map.64 = bf16[2,64,2048]{2,1,0:T(8,128)(2,1)} custom-call(s32[16]{0:T(128)} %target_ref.1, bf16[48,256]{1,0:T(8,128)(2,1)} %pad_maximum_fusion.feat_ref, bf16[64,2,2048]{2,1,0:T(2,128)(2,1)} %pairs_ref.1, bf16[3,256,2048]{2,1,0:T(8,128)(2,1)} %bitcast.8, bf16[3,2048,128]{2,1,0:T(8,128)(2,1)} %bitcast.10, bf16[128,2048]{1,0:T(8,128)(2,1)} %bitcast.11), custom_call_target="tpu_custom_call" | custom-call | tf_op jit(solution)/shard_map/pallas_call | solution.py:425
  80.6 2.4 %copy.7 = bf16[64,2,2048]{2,1,0:T(2,128)(2,1)} copy(bf16[64,2,2048]{2,0,1:T(8,128)(2,1)} %bitcast.9) | data formatting | bytes 1048576 | tf_op jit(solution)/shard_map/transpose | solution.py:466
  (2 shorter events, 0.0 us)
